TPU v7x, 512 devices: a whole 4x4x16 slice. The times are simulated.
512 devices in a mesh: rows: 32 (over x_lo, z), ka: 16 (over x_hi, y, core).
Axes of the slice: x: 4 (x_hi: 2, x_lo: 2; x = x_hi * 2 + x_lo), y: 4, z: 16, core: 2. Of those that a mesh axis runs over, the one named last changes fastest.
Arguments:
- pair_repr: bfloat16 [512, 512, 128], P('rows', 'ka'), may hold values from -6 to 6
- pair_mask: int32 [512, 512], P('rows', 'ka'), may hold values 0 or 1
- ln_gain: float32 [128], replicated, may hold values from 0.1 to 1.9
- ln_bias: float32 [128], replicated, may hold values from -3 to 3
- w_proj: bfloat16 [128, 256], replicated, may hold values from -0.5 to 0.5
- w_gate: bfloat16 [128, 256], replicated, may hold values from -0.5 to 0.5
- w_out_gate: bfloat16 [128, 128], replicated, may hold values from -0.5 to 0.5
- out_gain: float32 [128], replicated, may hold values from 0.1 to 1.9
- out_bias: float32 [128], replicated, may hold values from -3 to 3
- w_out: bfloat16 [128, 128], replicated, may hold values from -0.5 to 0.5
Outputs:
- update: bfloat16 [512, 512, 128], P('rows', 'ka')
All inputs are finite; a program needn't handle non-finite values. No bound on the sum of `pair_mask` on one device may be relied on, other than what follows from the above.
Results may differ from a plain program's by a relative error of at most 0.015.
Values may be sent and summed in bfloat16 or wider, within the bound.
A program may use at most 64 MiB of HBM per device.

v0:
```python
import jax
import jax.numpy as jnp
from jax import lax
from jax.sharding import Mesh
from jax.sharding import PartitionSpec as P

ROWS = ("rows_0", "rows_1")
KA = ("ka_0", "ka_1", "ka_2")


def joined_along(blocks, dim):
    blocks = jnp.moveaxis(blocks, 0, dim)
    dims = blocks.shape
    return blocks.reshape(*dims[:dim], dims[dim] * dims[dim + 1], *dims[dim + 2 :])


def stacked_from(array, axes, order):
    blocks = array[None]
    for k in order:
        blocks = lax.all_gather(blocks, axes[k], axis=0, tiled=True)
    carried = [lax.axis_size(axes[k]) for k in reversed(order)]
    blocks = blocks.reshape(*carried, *array.shape)
    turned = sorted(range(len(order)), key=lambda place: order[len(order) - 1 - place])
    return blocks.transpose(*turned, *range(len(order), blocks.ndim)).reshape(-1, *array.shape)


def whole_of(array, axes, order, dim):
    return joined_along(stacked_from(array, axes, order), dim)


def split_up(array, dim, count):
    dims = array.shape
    blocks = array.reshape(*dims[:dim], count, dims[dim] // count, *dims[dim + 1 :])
    return jnp.moveaxis(blocks, dim, 0)


def sum_at_owner(array, axis, dim):
    blocks = split_up(array, dim, lax.axis_size(axis))
    arrived = lax.all_to_all(blocks, axis, split_axis=0, concat_axis=0, tiled=True)
    return arrived.astype(jnp.float32).sum(axis=0)


def sum_in_two_steps(array, axes, dim):
    far, near = axes
    blocks = split_up(array, dim, lax.axis_size(far))
    nearer = sum_at_owner(blocks, near, dim + 1)
    arrived = lax.all_to_all(
        nearer.astype(jnp.bfloat16), far, split_axis=0, concat_axis=0, tiled=True
    )
    return arrived.astype(jnp.float32).sum(axis=0)


def layer_norm(values, gain_vec, bias_vec):
    center = jnp.mean(values, axis=-1, keepdims=True)
    deviate = values - center
    spread = jnp.mean(deviate * deviate, axis=-1, keepdims=True)
    return deviate * lax.rsqrt(spread + 1e-05) * gain_vec + bias_vec


def panel_sums(left_edge, right_edge):
    return jnp.einsum(
        "ikh,jkh->ijh",
        left_edge,
        whole_of(right_edge, ROWS, (0, 1), 0),
        preferred_element_type=jnp.float32,
    )


def body(
    pair_repr, pair_mask, ln_gain, ln_bias, w_proj, w_gate, w_out_gate, out_gain, out_bias, w_out
):
    row_count, col_count, chans = pair_repr.shape
    hidden = w_out.shape[0]
    normed = layer_norm(pair_repr.astype(jnp.float32), ln_gain, ln_bias).astype(jnp.bfloat16)
    flat_rows = normed.reshape(row_count * col_count, chans)
    projected = jnp.dot(flat_rows, w_proj, preferred_element_type=jnp.float32)
    gate_logits = jnp.dot(flat_rows, w_gate, preferred_element_type=jnp.float32)
    mask_col = pair_mask.reshape(row_count * col_count, 1).astype(jnp.float32)
    edges = (jax.nn.sigmoid(gate_logits) * projected * mask_col).astype(jnp.bfloat16)
    edges = edges.reshape(row_count, col_count, 2 * hidden)
    left_edge = edges[:, :, :hidden]
    right_edge = edges[:, :, hidden:]
    partial_sums = panel_sums(left_edge, right_edge)
    triangle = sum_in_two_steps(partial_sums.astype(jnp.bfloat16), (("ka_0", "ka_1"), "ka_2"), 1)
    tri_normed = layer_norm(triangle, out_gain, out_bias).astype(jnp.bfloat16)
    out_gate = jax.nn.sigmoid(jnp.dot(flat_rows, w_out_gate, preferred_element_type=jnp.float32))
    projected_out = jnp.dot(
        tri_normed.reshape(row_count * col_count, hidden), w_out, preferred_element_type=jnp.float32
    )
    return (out_gate * projected_out).astype(jnp.bfloat16).reshape(row_count, col_count, chans)


def solution(mesh):
    torus = Mesh(mesh.devices.reshape(2, 16, 2, 4, 2), ("rows_0", "rows_1", "ka_0", "ka_1", "ka_2"))
    placed = (P(ROWS, KA, None), P(ROWS, KA), P(), P(), P(), P(), P(), P(), P(), P())
    return jax.shard_map(
        body, mesh=torus, in_specs=placed, out_specs=P(ROWS, KA, None), check_vma=False
    )
```

profile of v0, /device:TPU:1, one launch (start us, length us, event | category | flops | bytes accessed | tf_op | source)
XLA Modules:
  0.0 160.7 jit_solution(4884521978984217984)
XLA Ops:
  6.5 0.0 copy-start
  6.5 0.0 all-gather.3.cloned.1.call-start
  6.5 1.1 convert_reduce_fusion.2
  7.6 1.2 fusion.11
  8.8 0.7 convert_element_type.40
  9.5 0.1 convert_element_type.41
  9.6 1.1 fusion.14
  10.7 0.0 copy-done
  10.7 0.3 fusion.2
  11.0 1.1 fusion.4
  12.2 5.1 %all-gather = bf16[32,32,128]{2,1,0:T(8,128)(2,1)} all-gather(bf16[16,32,128]{2,1,0:T(8,128)(2,1)S(1)} %get-tuple-element.7), channel_id=2, replica_groups=mesh['rows_0'=2,'rows_1'=16,'ka_0'=2,'ka_1'=4,'ka_2'=2] {'rows_0'}, dimensions={0}, use_global_device_ids=true | all-gather | bytes 393216 | tf_op jit(solution)/shard_map/all_gather | solution.py:20
  17.3 0.0 all-gather.3.cloned.1.call-update
  17.3 0.4 copy.30
  17.8 75.1 %all-gather.3.cloned.1.call-done = bf16[32,16,32,128]{3,2,1,0:T(8,128)(2,1)} async-done(((bf16[2,16,32,128]{3,2,1,0:T(8,128)(2,1)}), bf16[32,16,32,128]{3,2,1,0:T(8,128)(2,1)}) %all-gather.3.cloned.1.call-update) | async-done | bytes 4194320 | tf_op jit(solution)/shard_map/all_gather | solution.py:20
  92.9 5.3 %copy.23 = bf16[2,16,16,32,128]{4,3,2,1,0:T(8,128)(2,1)} copy(bf16[2,16,16,32,128]{4,3,2,0,1:T(8,128)(2,1)} %bitcast.39) | data formatting | bytes 8388608 | tf_op jit(solution)/shard_map/transpose | solution.py:24
  98.2 8.6 %copy.25 = bf16[512,32,128]{0,1,2:T(8,128)(2,1)} copy(bf16[512,32,128]{2,1,0:T(8,128)(2,1)} %bitcast.37) | data formatting | bytes 8388608 | tf_op jit(solution)/shard_map/reshape;reshape | solution.py:14
  106.9 2.9 %convert_bitcast_fusion = bf16[16,512,128]{1,0,2:T(8,128)(2,1)S(1)} fusion(bf16[16,32,128]{1,0,2:T(8,128)(2,1)S(1)} %copy.30, bf16[512,32,128]{0,1,2:T(8,128)(2,1)} %copy.25), kind=kOutput, calls=%fused_computation.2 | convolution fusion | flops 68157440 | bytes 6422528 | tf_op jit(solution)/shard_map/ikh,jkh->ijh/dot_general | solution.py:61
  109.7 3.1 %copy.26 = bf16[16,512,128]{2,1,0:T(8,128)(2,1)} copy(bf16[16,512,128]{1,0,2:T(8,128)(2,1)S(1)} %convert_bitcast_fusion) | data formatting | bytes 4194304 | tf_op jit(solution)/shard_map/convert_element_type | solution.py:84
  112.8 2.1 %copy.28 = bf16[2,8,16,32,128]{4,3,2,1,0:T(8,128)(2,1)S(1)} copy(bf16[2,8,16,32,128]{4,3,0,1,2:T(8,128)(2,1)} %bitcast.38) | data formatting | bytes 4194304 | tf_op jit(solution)/shard_map/transpose | solution.py:34
  115.0 0.0 copy-start.4
  115.0 14.5 %all_to_all.10 = bf16[2,8,16,32,128]{4,3,2,1,0:T(8,128)(2,1)S(1)} all-to-all(bf16[2,8,16,32,128]{4,3,2,1,0:T(8,128)(2,1)S(1)} %copy.28), channel_id=1, replica_groups=mesh['rows_0'=2,'rows_1'=16,'ka_0'=2,'ka_1'=4,'ka_2'=2] {'ka_2'}, dimensions={0} | all-to-all | bytes 4194304 | tf_op jit(solution)/shard_map/all_to_all | solution.py:39
  129.5 0.0 copy-start.2
  129.5 0.0 copy-start.3
  129.5 0.0 copy-start.1
  129.5 1.7 %reduce_sum.61 = bf16[8,16,32,128]{3,2,1,0:T(8,128)(2,1)} reduce(bf16[2,8,16,32,128]{4,3,2,1,0:T(8,128)(2,1)S(1)} %all_to_all.10, bf16[]{:T(256)} %constant.14.clone.1), dimensions={0}, to_apply=%region_2.0 | reduce | flops 524288 | bytes 3145730 | tf_op jit(solution)/shard_map/reduce_sum | solution.py:40
  131.1 6.4 %all-to-all-start.1 = ((bf16[8,16,32,128]{3,2,1,0:T(8,128)(2,1)}), bf16[8,16,32,128]{3,2,1,0:T(8,128)(2,1)S(1)}, u32[]{:S(2)}, u32[]{:S(2)}) async-start(bf16[8,16,32,128]{3,2,1,0:T(8,128)(2,1)} %reduce_sum.61), calls=%async_computation.1 | async-start | bytes 2097152 | tf_op jit(solution)/shard_map/all_to_all | solution.py:47
  137.6 0.0 copy-done.4
  137.6 0.2 fusion.7
  137.8 14.3 %all-to-all-done.1 = bf16[8,16,32,128]{3,2,1,0:T(8,128)(2,1)S(1)} async-done(((bf16[8,16,32,128]{3,2,1,0:T(8,128)(2,1)}), bf16[8,16,32,128]{3,2,1,0:T(8,128)(2,1)S(1)}, u32[]{:S(2)}, u32[]{:S(2)}) %all-to-all-start.1) | async-done | bytes 1048608 | tf_op jit(solution)/shard_map/all_to_all | solution.py:47
  152.1 0.2 convert_reduce_fusion
  152.3 0.1 div.25
  152.4 0.3 multiply_reduce_fusion
  152.7 0.1 rsqrt.21
  152.8 0.0 copy-done.2
  152.8 0.0 copy-done.3
  152.8 0.2 fusion.18
  153.0 0.0 copy-done.1
  153.0 0.8 fusion.8
  (5 shorter events, 0.1 us)
Async XLA Ops:
  6.5 4.2 %copy-start = (bf16[128,256]{1,0:T(8,128)(2,1)S(1)}, bf16[128,256]{1,0:T(8,128)(2,1)}, u32[]{:S(2)}) copy-start(bf16[128,256]{1,0:T(8,128)(2,1)} %param.15) | copy-start | bytes 196612
  6.5 86.3 %all-gather.3.cloned.1.call-start = ((), (), s32[]{:S(2)}) async-start(), calls=%async_computation.2 | async-start | bytes 4456448 | tf_op jit(solution)/shard_map/all_gather | solution.py:20
  115.0 22.6 %copy-start.4 = (bf16[128,128]{1,0:T(8,128)(2,1)S(1)}, bf16[128,128]{1,0:T(8,128)(2,1)}, u32[]{:S(2)}) copy-start(bf16[128,128]{1,0:T(8,128)(2,1)} %param.16) | copy-start | bytes 98308
  129.5 23.3 %copy-start.2 = (f32[128]{0:T(128)S(1)}, f32[128]{0:T(128)}, u32[]{:S(2)}) copy-start(f32[128]{0:T(128)} %param.18) | copy-start | bytes 1540
  129.5 23.3 %copy-start.3 = (f32[128]{0:T(128)S(1)}, f32[128]{0:T(128)}, u32[]{:S(2)}) copy-start(f32[128]{0:T(128)} %param.17) | copy-start | bytes 1540
  129.5 23.5 %copy-start.1 = (bf16[128,128]{1,0:T(8,128)(2,1)S(1)}, bf16[128,128]{1,0:T(8,128)(2,1)}, u32[]{:S(2)}) copy-start(bf16[128,128]{1,0:T(8,128)(2,1)} %param.19) | copy-start | bytes 98308
  131.1 20.9 %all-to-all-start.1 = ((bf16[8,16,32,128]{3,2,1,0:T(8,128)(2,1)}), bf16[8,16,32,128]{3,2,1,0:T(8,128)(2,1)S(1)}, u32[]{:S(2)}, u32[]{:S(2)}) async-start(bf16[8,16,32,128]{3,2,1,0:T(8,128)(2,1)} %reduce_sum.61), calls=%async_computation.1 | async-start | bytes 2097152 | tf_op jit(solution)/shard_map/all_to_all | solution.py:47
Sparse Core Ops, SparseCore 0:
  17.4 75.3 all-gather.2
where the time goes:
time: 161 us
  waiting for transfers between devices  89.4 us (56%)
  local copies, waits for them, and re-layouts  20 us (12%)
  blocking collectives  19.6 us (12%)
  between operations  13.5 us (8%)
  other arithmetic  6.43 us (4%)
  starting transfers between devices  6.42 us (4%)
  matrix products  5.27 us (3%)
    all_gather x1, waiting for transfers between devices, stacked_from(): blocks = lax.all_gather(blocks, axes[k], axis=0, tiled=True)  75.1 us
    all_to_all x1, blocking collectives, sum_at_owner(): lax.all_to_all(blocks, axis, split_axis=0, concat_axis=0, tiled=True)  14.5 us
    all_to_all x1, waiting for transfers between devices, sum_in_two_steps(): lax.all_to_all(nearer.astype(jnp.bfloat16), far, split_axis=0, concat_axi...  14.3 us
    another operation x1, local copies, waits for them, and re-layouts, joined_along(): blocks.reshape(*dims[:dim], dims[dim] * dims[dim + 1], *dims[dim + 2:])  8.64 us
    all_to_all x1, starting transfers between devices, sum_in_two_steps(): lax.all_to_all(nearer.astype(jnp.bfloat16), far, split_axis=0, concat_axi...  6.41 us
    transpose x1, local copies, waits for them, and re-layouts, stacked_from(): blocks.transpose(*turned, *range(len(order), blocks.ndim))  5.33 us
    all_gather x1, blocking collectives, stacked_from(): blocks = lax.all_gather(blocks, axes[k], axis=0, tiled=True)  5.13 us
  transfers between devices with their start and end apart: 2, of which 2 were waited for; matrix products, arithmetic and copies ran while one was open for 0% of the time, Pallas kernels for 0%

commit v1 on v0

v1 whole, which is shorter than its diff:
```python
import jax
import jax.numpy as jnp
from jax import lax
from jax.experimental import pallas as pl
from jax.experimental.pallas import tpu as pltpu
from jax.sharding import PartitionSpec as P

MESH = pl.DeviceIdType.MESH
F32 = jnp.float32
BF16 = jnp.bfloat16
NT = (((1,), (1,)), ((), ()))
ZN = 16
PLANE = 32
KAN = 16
EPS = 1e-05


def iota(shape, dim):
    return lax.broadcasted_iota(jnp.int32, shape, dim)


def dot_nt(a, b):
    return lax.dot_general(a, b, NT, preferred_element_type=F32)


def chunk_swap(tiles, chunk):
    for bit, width in ((1, 32), (2, 64)):
        low = (chunk & bit) == 0
        swapped = []
        for e in range(4):
            other = tiles[e ^ bit]
            if e & bit:
                swapped.append(jnp.where(low, pltpu.roll(other, 128 - width, 1), tiles[e]))
            else:
                swapped.append(jnp.where(low, tiles[e], pltpu.roll(other, width, 1)))
        tiles = swapped
    return tiles


def kernel(
    pair, mask, gain, bias, w_proj, w_gate, w_out_gate, out_gain, out_bias, w_out, out,
    normed, stage, send_r, send_l, recv_l, ring, left_m, right_m, packed, send_o, recv_o,
    gate_s, gain_t, bias_t, flat,
    sem_r, sem_rs, sem_l, sem_ls, sem_ring, sem_up, sem_dn, sem_o, sem_os,
):
    rows = lax.axis_index("rows")
    ka = lax.axis_index("ka")
    xlo = rows // ZN
    z = rows % ZN
    me = xlo * KAN + ka
    mine_c = ka // 4
    mine_s = xlo * 4 + ka % 4
    up = {"rows": xlo * ZN + (z + 1) % ZN, "ka": ka}
    down = {"rows": xlo * ZN + (z + ZN - 1) % ZN, "ka": ka}

    def peer(t):
        d = (me + t) % PLANE
        return d, {"rows": (d // KAN) * ZN + z, "ka": d % KAN}

    barrier = pltpu.get_barrier_semaphore()

    @pl.loop(1, PLANE)
    def _(t):
        pl.semaphore_signal(barrier, inc=1, device_id=peer(t)[1], device_id_type=MESH)

    pl.semaphore_signal(barrier, inc=1, device_id=up, device_id_type=MESH)
    pl.semaphore_signal(barrier, inc=1, device_id=down, device_id_type=MESH)

    spread = (iota((32, 128), 1) % 32 == iota((32, 128), 0)).astype(BF16)
    wide = jnp.dot(mask[...].astype(F32).astype(BF16), spread, preferred_element_type=F32)
    wide = jnp.where(iota((16, 128), 1) // 32 == iota((16, 128), 0) % 4, wide, 0.0)
    group = (iota((8, 16), 1) // 4 == iota((8, 16), 0)).astype(BF16)
    mask_rows = jnp.dot(group, wide.astype(BF16), preferred_element_type=F32)

    for a in range(4):
        x = pair[4 * a : 4 * a + 4].reshape(128, 128).astype(F32)
        d = x - jnp.mean(x, axis=1, keepdims=True)
        v = jnp.mean(d * d, axis=1, keepdims=True)
        normed[128 * a : 128 * a + 128, :] = (d * lax.rsqrt(v + EPS) * gain[...] + bias[...]).astype(BF16)

    def edges(lo, send):
        wp = w_proj[:, lo : lo + 128].astype(F32).T.astype(BF16)
        wg = w_gate[:, lo : lo + 128].astype(F32).T.astype(BF16)
        for a in range(4):
            n = normed[128 * a : 128 * a + 128, :]
            e = jax.nn.sigmoid(dot_nt(wg, n)) * dot_nt(wp, n) * mask_rows[a : a + 1, :]
            stage[pl.ds(a, 128, stride=4), :] = e
        send[...] = stage[...].reshape(PLANE, 16, 128).astype(BF16)

    def exchange(send, landing, send_sem, recv_sem):
        @pl.loop(1, PLANE)
        def _(t):
            d, device = peer(t)
            pltpu.make_async_remote_copy(
                src_ref=send.at[d], dst_ref=landing, send_sem=send_sem, recv_sem=recv_sem,
                device_id=device, device_id_type=MESH,
            ).start()

        pltpu.make_async_copy(send.at[me], landing, recv_sem).start()

    edges(128, send_r)
    pl.semaphore_wait(barrier, PLANE + 1)
    exchange(send_r, ring.at[z, mine_c, mine_s], sem_rs, sem_r.at[mine_c])
    edges(0, send_l)
    exchange(send_l, recv_l.at[mine_c, mine_s], sem_ls, sem_l)

    def hop(block, c, sem, device):
        return pltpu.make_async_remote_copy(
            src_ref=ring.at[block, c], dst_ref=ring.at[block, c], send_sem=sem,
            recv_sem=sem_ring.at[block, c], device_id=device, device_id_type=MESH,
        )

    for c in range(4):
        pltpu.make_async_copy(ring.at[z, c], ring.at[z, c], sem_r.at[c]).wait()
        hop(z, c, sem_up, up).start()
        hop(z, c, sem_dn, down).start()

    chunk = iota((16, 128), 1) // 32

    def relay(tiles, place):
        tiles = tiles.astype(F32)
        for x in range(2):
            for b, t in enumerate(chunk_swap([tiles[4 * x + e] for e in range(4)], chunk)):
                place(x, b, t.astype(BF16))

    def relay_right(side, block, c):
        def place(x, b, t):
            row = 16 * (4 * x + b)
            right_m[side, row : row + 16, 128 * c : 128 * c + 128] = t

        relay(ring[block, c], place)

    row8 = iota((8, 128), 0)
    slot = (iota((8, 128), 1) // 4) % 4
    lane_low = iota((32, 128), 1) < 64

    def products(side, block):
        prod = dot_nt(left_m[...], right_m[side])
        for v in range(4):
            total = jnp.zeros((8, 128), F32)
            for b in range(4):
                piece = prod[32 * b + 8 * v : 32 * b + 8 * v + 8]
                for half in range(2):
                    h = 2 * (v % 2) + half
                    moved = piece if b == h else pltpu.roll(piece, (4 * (b - h)) % 128, 1)
                    total = jnp.where((row8 // 4 == half) & (slot == b), moved, total)
            packed[block, 8 * v : 8 * v + 8, :] = total

    def send_pair(t):
        odd = (z + t) % 2
        q = ((odd * (z + t) + (1 - odd) * (z - t + ZN)) % ZN) // 2
        even_p = packed[2 * q]
        odd_p = packed[2 * q + 1]
        sends = (
            jnp.where(lane_low, even_p, pltpu.roll(odd_p, 64, 1)),
            jnp.where(lane_low, pltpu.roll(even_p, 64, 1), odd_p),
        )
        for xj in range(2):
            for xi in range(2):
                at = 4 * q + 2 * xj + xi
                send_o[at] = sends[xj][16 * xi : 16 * xi + 16].astype(BF16)
        for xj in range(2):
            for xi in range(2):
                at = 4 * q + 2 * xj + xi
                target = xi * KAN + xj * 8 + q

                @pl.when(target != me)
                def _():
                    pltpu.make_async_remote_copy(
                        src_ref=send_o.at[at], dst_ref=recv_o.at[me], send_sem=sem_os, recv_sem=sem_o,
                        device_id={"rows": xi * ZN + z, "ka": xj * 8 + q}, device_id_type=MESH,
                    ).start()

                @pl.when(target == me)
                def _():
                    pltpu.make_async_copy(send_o.at[at], recv_o.at[me], sem_o).start()

    for c in range(4):
        relay_right(0, z, c)
    pltpu.make_async_copy(recv_l, recv_l, sem_l).wait()
    for c in range(4):
        def place(x, b, t):
            row = 16 * (2 * b + x)
            left_m[row : row + 16, 128 * c : 128 * c + 128] = t

        relay(recv_l[c], place)
    products(0, z)

    gain_t[...] = jnp.broadcast_to(out_gain[...], (128, 128)).T
    bias_t[...] = jnp.broadcast_to(out_bias[...], (128, 128)).T
    gate_s[...] = jax.nn.sigmoid(jnp.dot(normed[...], w_out_gate[...], preferred_element_type=F32))

    @pl.loop(1, 8)
    def _(t):
        zu = (z - t + ZN) % ZN
        zd = (z + t) % ZN
        for c in range(4):
            hop(zu, c, sem_up, up).wait_recv()
            if c < 2:
                hop(zu, c, sem_up, up).start()
            else:
                @pl.when(t < 7)
                def _():
                    hop(zu, c, sem_up, up).start()
            hop(zd, c, sem_dn, down).wait_recv()
            if c >= 2:
                hop(zd, c, sem_dn, down).start()
            else:
                @pl.when(t < 7)
                def _():
                    hop(zd, c, sem_dn, down).start()
            relay_right(0, zu, c)
            relay_right(1, zd, c)
        products(0, zu)
        products(1, zd)
        send_pair(t)

    far = (z + 8) % ZN
    for c in range(4):
        hop(far, c, sem_up, up).wait_recv()
        relay_right(0, far, c)
    products(0, far)
    send_pair(8)

    r = iota((128, 128), 0)
    source = ((r // 16) % 2) * 64 + (r % 4) * 16 + (r // 32) * 4 + (r // 4) % 4
    turn = (iota((128, 128), 1) == source).astype(F32).astype(BF16)

    pltpu.make_async_copy(recv_o, recv_o, sem_o).wait()
    flat[...] = recv_o[...].reshape(512, 128).astype(F32)
    for a in range(4):
        y = flat[pl.ds(a, 128, stride=4), :]
        d = y - jnp.mean(y, axis=0, keepdims=True)
        v = jnp.mean(d * d, axis=0, keepdims=True)
        n = (d * lax.rsqrt(v + EPS) * gain_t[...] + bias_t[...]).astype(BF16)
        turned = dot_nt(turn, n).astype(BF16)
        proj = jnp.dot(turned, w_out[...], preferred_element_type=F32)
        result = (gate_s[128 * a : 128 * a + 128, :] * proj).astype(BF16)
        out[4 * a : 4 * a + 4] = result.reshape(4, 32, 128)

    pltpu.make_async_copy(send_r.at[pl.ds(0, 31)], send_r.at[pl.ds(0, 31)], sem_rs).wait()
    pltpu.make_async_copy(send_l.at[pl.ds(0, 31)], send_l.at[pl.ds(0, 31)], sem_ls).wait()
    pltpu.make_async_copy(send_o.at[pl.ds(0, 31)], send_o.at[pl.ds(0, 31)], sem_os).wait()
    sent = ring.at[pl.ds(0, 15), pl.ds(0, 2)]
    pltpu.make_async_copy(sent, sent, sem_up).wait()
    pltpu.make_async_copy(sent, sent, sem_dn).wait()


def body(
    pair_repr, pair_mask, ln_gain, ln_bias, w_proj, w_gate, w_out_gate, out_gain, out_bias, w_out
):
    dma = pltpu.SemaphoreType.DMA
    vmem = pl.BlockSpec(memory_space=pltpu.VMEM)
    row = lambda v: v.reshape(1, 128)
    return pl.pallas_call(
        kernel,
        out_shape=jax.ShapeDtypeStruct((16, 32, 128), BF16),
        in_specs=[vmem] * 10,
        out_specs=vmem,
        scratch_shapes=[
            pltpu.VMEM((512, 128), BF16),
            pltpu.VMEM((512, 128), F32),
            pltpu.VMEM((PLANE, 16, 128), BF16),
            pltpu.VMEM((PLANE, 16, 128), BF16),
            pltpu.VMEM((4, 8, 16, 128), BF16),
            pltpu.VMEM((ZN, 4, 8, 16, 128), BF16),
            pltpu.VMEM((128, 512), BF16),
            pltpu.VMEM((2, 128, 512), BF16),
            pltpu.VMEM((ZN, 32, 128), F32),
            pltpu.VMEM((PLANE, 16, 128), BF16),
            pltpu.VMEM((PLANE, 16, 128), BF16),
            pltpu.VMEM((512, 128), F32),
            pltpu.VMEM((128, 128), F32),
            pltpu.VMEM((128, 128), F32),
            pltpu.VMEM((512, 128), F32),
            dma((4,)),
            dma,
            dma,
            dma,
            dma((ZN, 4)),
            dma,
            dma,
            dma,
            dma,
        ],
        compiler_params=pltpu.CompilerParams(collective_id=0, has_side_effects=True),
        name="triangle",
    )(
        pair_repr, pair_mask, row(ln_gain), row(ln_bias), w_proj, w_gate, w_out_gate,
        row(out_gain), row(out_bias), w_out,
    )


def solution(mesh):
    spread = P("rows", "ka", None)
    placed = (spread, P("rows", "ka")) + (P(),) * 8
    return jax.shard_map(body, mesh=mesh, in_specs=placed, out_specs=spread, check_vma=False)
```

time: 161 us -> 57.1 us (0.35)
  the two profiles are of different devices: /device:TPU:1 before, /device:TPU:16 now
where the time goes in v1:
time: 57.1 us; the launch traced here: 57 us
  Pallas kernels  55.4 us (97%)
  local copies, waits for them, and re-layouts  1.57 us (3%)
    pallas_call x1, Pallas kernels, body(): pl.pallas_call(kernel, out_shape=jax.ShapeDtypeStruct((16, 32, 128), BF16...  55.4 us
    unnamed x1, local copies, waits for them, and re-layouts  1.57 us

profile of v1, /device:TPU:16, one launch (start us, length us, event | category | flops | bytes accessed | tf_op | source)
XLA Modules:
  0.0 57.0 jit_solution(1091235621234388901)
XLA Ops:
  0.0 55.4 %triangle.1 = bf16[16,32,128]{2,1,0:T(8,128)(2,1)} custom-call(bf16[16,32,128]{2,1,0:T(8,128)(2,1)} %pair.1, s32[16,32]{1,0:T(8,128)} %mask.1, f32[1,128]{1,0:T(1,128)} %bitcast.4, f32[1,128]{1,0:T(1,128)} %bitcast.5, bf16[128,256]{1,0:T(8,128)(2,1)} %w_proj.1, bf16[128,256]{1,0:T(8,128)(2,1)} %w_gate.1, bf16[128,128]{1,0:T(8,128)(2,1)} %w_out_gate.1, ...), custom_call_target="tpu_custom_call" | custom-call | tf_op jit(solution)/shard_map/triangle/pallas_call | solution.py:255
  55.4 1.6 %copy.12 = bf16[16,32,128]{2,1,0:T(8,128)(2,1)} copy(bf16[16,32,128]{2,1,0:T(8,128)(2,1)} %triangle.1) | data formatting | bytes 262144
